TPU v7x, 32 devices: a whole 2x2x4 slice. The times are simulated.
32 devices in a mesh: radial: 8 (over z, x), phi: 4 (over y, core).
Axes of the slice: x: 2, y: 2, z: 4, core: 2. Of those that a mesh axis runs over, the one named last changes fastest.
Arguments:
- conserved: float32 [8, 64, 64, 128], P(None, 'radial', 'phi'), may hold values from -2.5 to 7, as said below
- core_mass: float32 [1], replicated, may hold values from 0.2 to 1
Outputs:
- advanced: float32 [8, 64, 64, 128], P(None, 'radial', 'phi')
- enclosed_mass: float32 [64], P('radial')
Inputs may be any that keep to these rules, and one draw needn't show every extreme that they name: conserved[0] (density) lies between 0.4 and 2.5; conserved[4] exceeds (conserved[1]^2 + conserved[2]^2 + conserved[3]^2)/(2 conserved[0]) by at least 0.6; the speeds |conserved[m]/conserved[0]| stay below 1; conserved[5..7] lie between 0 and conserved[0].
All inputs are finite; a program needn't handle non-finite values.
Results may differ from a plain program's by a relative error of at most 0.0003.
Values sent between devices are 32-bit elements; how exact they have to be, the bound alone decides.
A program may use at most 64 MiB of HBM per device.

v0:
```python
import math
import jax
import jax.numpy as jnp
from jax import lax
from jax.sharding import PartitionSpec as P

ADIABATIC = 4.0 / 3.0
INNER_RADIUS = 1.0
OUTER_RADIUS = 2.0
COURANT = 0.4
GRAVITY_KICK = 0.004
MINIMUM_DENSITY = 0.05
PRESSURE_FLOOR = 0.01


def entering(part, axis, combine, identity):
    place = lax.axis_index(axis)
    gathered = lax.all_gather(part, axis)
    state = jnp.zeros_like(part) + jnp.asarray(identity, part.dtype)

    def one(lap, state):
        return combine(state, lax.dynamic_index_in_dim(gathered, lap, 0, False))

    return lax.fori_loop(0, place, one, state)


def extended_2(value, sides, width, wrap):
    for axis, dim in sides:
        peers, length = (lax.axis_size(axis), value.shape[dim])
        up = [(i, (i + 1) % peers) for i in range(peers if wrap else peers - 1)]
        down = [(j, i) for i, j in up]
        last = lax.slice_in_dim(value, length - width, length, axis=dim)
        initial = lax.slice_in_dim(value, 0, width, axis=dim)
        before = lax.ppermute(last, axis, up)
        after = lax.ppermute(initial, axis, down)
        value = jnp.concatenate([before, value, after], axis=dim)
    return value


def step_sizes(radial_total, phi_total, theta_total):
    theta_step = math.pi / theta_total
    phi_step = 2.0 * math.pi / phi_total
    polar_width = INNER_RADIUS * math.sin(0.5 * theta_step) * phi_step
    radial_step = min(2.0 * polar_width, (OUTER_RADIUS - INNER_RADIUS) / radial_total)
    timestep = COURANT * min(radial_step, polar_width)
    return (radial_step, theta_step, phi_step, timestep)


def thermo(values):
    density = jnp.maximum(values[0], MINIMUM_DENSITY)
    kinetic = (
        0.5 * (values[1] * values[1] + values[2] * values[2] + values[3] * values[3]) / density
    )
    pressure = jnp.maximum((ADIABATIC - 1.0) * (values[4] - kinetic), PRESSURE_FLOOR * density)
    return (density, pressure)


def physical(values, component):
    density, pressure = thermo(values)
    normal = values[component] / density
    sound = jnp.sqrt(ADIABATIC * pressure / density)
    pieces = [values[which] * normal for which in range(values.shape[0])]
    pieces[component] = pieces[component] + pressure
    pieces[4] = pieces[4] + pressure * normal
    return (jnp.stack(pieces), jnp.abs(normal) + sound)


def face_flux(values, along_dim, component):
    interior = values.shape[along_dim] - 4
    neighbour_differences = lax.slice_in_dim(
        values, 1, interior + 4, axis=along_dim
    ) - lax.slice_in_dim(values, 0, interior + 3, axis=along_dim)
    below_diff = lax.slice_in_dim(neighbour_differences, 0, interior + 2, axis=along_dim)
    above_diff = lax.slice_in_dim(neighbour_differences, 1, interior + 3, axis=along_dim)
    limited = (
        0.5
        * (jnp.sign(below_diff) + jnp.sign(above_diff))
        * jnp.minimum(jnp.abs(below_diff), jnp.abs(above_diff))
    )
    left_state = lax.slice_in_dim(values, 1, interior + 2, axis=along_dim) + 0.5 * lax.slice_in_dim(
        limited, 0, interior + 1, axis=along_dim
    )
    right_state = lax.slice_in_dim(
        values, 2, interior + 3, axis=along_dim
    ) - 0.5 * lax.slice_in_dim(limited, 1, interior + 2, axis=along_dim)
    left_flux, left_signal = physical(left_state, component)
    right_flux, right_signal = physical(right_state, component)
    signal = jnp.maximum(left_signal, right_signal)
    return 0.5 * (left_flux + right_flux) - 0.5 * signal * (right_state - left_state)


def hydro_rate(extended, cell_centers, enclosed, radial_step, theta_step, phi_step, strength):
    theta_cells = extended.shape[3]
    centre_cells = extended[:, 2:-2, 2:-2, :]
    polar_padded = jnp.pad(centre_cells, ((0, 0), (0, 0), (0, 0), (2, 2)), mode="edge")
    radial_flux = face_flux(extended[:, :, 2:-2, :], 1, 1)
    polar_flux = face_flux(polar_padded, 3, 2)
    azimuth_flux = face_flux(extended[:, 2:-2, :, :], 2, 3)
    angles = (jnp.arange(theta_cells, dtype=jnp.float32) + 0.5) * theta_step
    sine_center = jnp.sin(angles)
    cosine = jnp.cos(angles)
    face_sine = jnp.sin(jnp.arange(theta_cells + 1, dtype=jnp.float32) * theta_step)
    radius = cell_centers[:, None, None]
    face_radius = jnp.concatenate(
        [cell_centers - 0.5 * radial_step, cell_centers[-1:] + 0.5 * radial_step]
    )[:, None, None]
    radial_area = face_radius * face_radius * radial_flux
    divergence = (radial_area[:, 1:] - radial_area[:, :-1]) / (radius * radius * radial_step)
    polar_area = face_sine * polar_flux
    divergence = divergence + (polar_area[..., 1:] - polar_area[..., :-1]) / (
        radius * sine_center * theta_step
    )
    divergence = divergence + (azimuth_flux[:, :, 1:] - azimuth_flux[:, :, :-1]) / (
        radius * sine_center * phi_step
    )
    density, pressure = thermo(centre_cells)
    radial_speed = centre_cells[1] / density
    polar_speed = centre_cells[2] / density
    azimuth_speed = centre_cells[3] / density
    cotangent = cosine / sine_center
    gravity_pull = strength * enclosed[:, None, None] / (radius * radius)
    source_radial = (
        2.0 * pressure + density * (polar_speed * polar_speed + azimuth_speed * azimuth_speed)
    ) / radius - density * gravity_pull
    source_polar = (
        pressure * cotangent
        + density * azimuth_speed * azimuth_speed * cotangent
        - density * radial_speed * polar_speed
    ) / radius
    source_azimuth = -density * azimuth_speed * (radial_speed + polar_speed * cotangent) / radius
    source_energy = -centre_cells[1] * gravity_pull
    nothing = jnp.zeros_like(pressure)
    source = jnp.stack(
        [
            nothing,
            source_radial,
            source_polar,
            source_azimuth,
            source_energy,
            nothing,
            nothing,
            nothing,
        ]
    )
    return source - divergence


def add_terms(earlier, later):
    return earlier + later


def body(conserved, core_mass):
    radial_rows = conserved.shape[1]
    phi_cells = conserved.shape[2]
    theta_cells = conserved.shape[3]
    radial_devices = lax.axis_size("radial")
    position = lax.axis_index("radial")
    radial_step, theta_step, phi_step, timestep = step_sizes(
        radial_rows * radial_devices, phi_cells * lax.axis_size("phi"), theta_cells
    )
    strength = GRAVITY_KICK / timestep
    first_row = position * radial_rows
    cell_centers = (
        INNER_RADIUS
        + ((first_row + jnp.arange(radial_rows, dtype=jnp.int32)).astype(jnp.float32) + 0.5)
        * radial_step
    )
    sine_center = jnp.sin((jnp.arange(theta_cells, dtype=jnp.float32) + 0.5) * theta_step)
    local_shells = jnp.dot(
        jnp.sum(conserved[0], axis=1), sine_center, precision=lax.Precision.HIGHEST
    )
    local_shells = (
        local_shells * cell_centers * cell_centers * (radial_step * theta_step * phi_step)
    )
    shells = lax.psum(local_shells, "phi")
    before = entering(jnp.sum(shells), "radial", add_terms, jnp.float32(0.0))
    enclosed = core_mass[0] + before + jnp.cumsum(shells) - 0.5 * shells

    def clipped_rows(extended, halo_width):
        total_rows = extended.shape[1]
        low_rows = jnp.where(
            position == 0,
            lax.slice_in_dim(extended, halo_width, halo_width + 1, axis=1),
            lax.slice_in_dim(extended, 0, halo_width, axis=1),
        )
        high_rows = jnp.where(
            position == radial_devices - 1,
            lax.slice_in_dim(
                extended, total_rows - halo_width - 1, total_rows - halo_width, axis=1
            ),
            lax.slice_in_dim(extended, total_rows - halo_width, total_rows, axis=1),
        )
        middle = lax.slice_in_dim(extended, halo_width, total_rows - halo_width, axis=1)
        return jnp.concatenate([low_rows, middle, high_rows], axis=1)

    def extend(values):
        wedge_split_state = extended_2(values, (("phi", 2),), 2, True)
        slab_split_state = extended_2(wedge_split_state, (("radial", 1),), 2, False)
        return clipped_rows(slab_split_state, 2)

    section_one = conserved + timestep * hydro_rate(
        extend(conserved), cell_centers, enclosed, radial_step, theta_step, phi_step, strength
    )
    section_two = section_one + timestep * hydro_rate(
        extend(section_one), cell_centers, enclosed, radial_step, theta_step, phi_step, strength
    )
    advanced = 0.5 * conserved + 0.5 * section_two
    return (advanced, enclosed)


def solution(mesh):
    in_specs = (P(None, "radial", "phi", None), P())
    out_specs = (P(None, "radial", "phi", None), P("radial"))
    return jax.shard_map(body, mesh=mesh, in_specs=in_specs, out_specs=out_specs, check_vma=False)
```

profile of v0, /device:TPU:24, one launch (start us, length us, event | category | flops | bytes accessed | tf_op | source)
XLA Modules:
  0.0 98.6 jit_solution(16917580335347414988)
XLA Ops:
  0.6 1.1 %fusion.53 = (f32[8,8,2,128]{3,2,1,0:T(2,128)S(1)}, f32[8,8,2,128]{3,2,1,0:T(2,128)S(1)}) fusion(f32[8,8,16,128]{3,2,1,0:T(8,128)} %param.4), kind=kLoop, calls=%fused_computation.338 | loop fusion | bytes 262144 | tf_op jit(solution)/shard_map/slice | solution.py:32
  1.8 0.6 copy.673
  2.4 0.6 copy.674
  3.0 1.7 %collective-permute-start.1 = (f32[8,8,2,128]{3,1,2,0:T(8,128)}, f32[8,8,2,128]{3,1,2,0:T(8,128)}, u32[]{:S(2)}, u32[]{:S(2)}) collective-permute-start(f32[8,8,2,128]{3,1,2,0:T(8,128)} %copy.674), channel_id=1, source_target_pairs={{1,0},{2,1},{3,2},{0,3},{5,4},{6,5},{7,6},{4,7},{9,8},{10,9},{11,1... | collective-permute-start | bytes 196616 | tf_op jit(solution)/shard_map/ppermute | solution.py:35
  4.8 0.6 multiply_multiply_fusion.4
  5.3 0.5 broadcast_add_fusion
  6.2 0.7 fusion.44
  6.9 0.6 constant_dynamic-update-slice_fusion.61
  7.5 0.4 copy.675
  7.9 0.4 copy.676
  8.8 0.5 pad_maximum_fusion.6
  9.3 0.3 slice_subtract_fusion.1
  9.6 0.7 minimum_multiply_fusion.1
  10.4 0.8 fusion.6
  11.1 0.2 multiply_bitcast_fusion.1
  11.8 0.8 copy-done.1
  12.6 1.0 copy-done.3
  13.6 0.7 fusion.2
  14.3 5.8 %psum.7 = f32[8]{0:T(128)S(1)} all-reduce(f32[8]{0:T(128)} %fusion.2), channel_id=1, replica_groups=mesh['radial'=8,'phi'=4] {'phi'}, use_global_device_ids=true, to_apply=%region_1.0 | all-reduce | flops 8 | bytes 64 | tf_op jit(solution)/shard_map/psum | solution.py:175
  20.0 0.6 reduce_sum.19
  20.6 1.3 %dynamic-slice = u32[1]{0:T(128)} dynamic-slice(u32[32]{0:T(128)} %constant.10, u32[]{:T(128)S(6)} %add.633), dynamic_slice_sizes={1} | dynamic-slice | bytes 12
  21.9 0.5 broadcast.552
  22.4 2.4 %dynamic-update-slice = f32[8]{0:T(128)} dynamic-update-slice(f32[8]{0:T(128)} %broadcast.552, f32[1]{0:T(128)} %bitcast.4, u32[]{:T(128)} %bitcast.5) | dynamic-update-slice | bytes 12
  24.8 0.6 slice.710
  25.4 17.5 %all-reduce = f32[8]{0:T(128)} all-reduce(f32[8]{0:T(128)} %dynamic-update-slice), channel_id=1, replica_groups=mesh['radial'=8,'phi'=4] {'radial'}, use_global_device_ids=true, to_apply=%add | all-reduce | flops 8 | bytes 64
  42.9 11.3 %while.10 = (s32[]{:T(128)}, f32[]{:T(128)}, s32[]{:T(128)}, f32[8]{0:T(128)}, s32[]{:T(128)}, /*index=5*/s32[]{:T(128)}, s32[]{:T(128)}) while((s32[]{:T(128)}, f32[]{:T(128)}, s32[]{:T(128)}, f32[8]{0:T(128)}, s32[]{:T(128)}, /*index=5*/s32[]{:T(128)}, s32[]{:T(128)}) %tuple.74), condition=%wide.region_4.5_spmd, body=%wide.region_3.4_spmd.sunk | while | flops 6 | bytes 135 | solution.py:24
  42.9 1.2 %dynamic_slice.5 = f32[1]{0:T(128)} dynamic-slice(f32[8]{0:T(128)} %get-tuple-element.163, s32[]{:T(128)S(6)} %select_n.41), dynamic_slice_sizes={1} | dynamic-slice | bytes 12 | tf_op jit(solution)/shard_map/while/body/jit(dynamic_index_in_dim)/dynamic_slice | solution.py:22
  44.8 1.2 %dynamic_slice.5 = f32[1]{0:T(128)} dynamic-slice(f32[8]{0:T(128)} %get-tuple-element.163, s32[]{:T(128)S(6)} %select_n.41), dynamic_slice_sizes={1} | dynamic-slice | bytes 12 | tf_op jit(solution)/shard_map/while/body/jit(dynamic_index_in_dim)/dynamic_slice | solution.py:22
  46.6 1.2 %dynamic_slice.5 = f32[1]{0:T(128)} dynamic-slice(f32[8]{0:T(128)} %get-tuple-element.163, s32[]{:T(128)S(6)} %select_n.41), dynamic_slice_sizes={1} | dynamic-slice | bytes 12 | tf_op jit(solution)/shard_map/while/body/jit(dynamic_index_in_dim)/dynamic_slice | solution.py:22
  48.5 1.2 %dynamic_slice.5 = f32[1]{0:T(128)} dynamic-slice(f32[8]{0:T(128)} %get-tuple-element.163, s32[]{:T(128)S(6)} %select_n.41), dynamic_slice_sizes={1} | dynamic-slice | bytes 12 | tf_op jit(solution)/shard_map/while/body/jit(dynamic_index_in_dim)/dynamic_slice | solution.py:22
  50.4 1.2 %dynamic_slice.5 = f32[1]{0:T(128)} dynamic-slice(f32[8]{0:T(128)} %get-tuple-element.163, s32[]{:T(128)S(6)} %select_n.41), dynamic_slice_sizes={1} | dynamic-slice | bytes 12 | tf_op jit(solution)/shard_map/while/body/jit(dynamic_index_in_dim)/dynamic_slice | solution.py:22
  52.3 1.2 %dynamic_slice.5 = f32[1]{0:T(128)} dynamic-slice(f32[8]{0:T(128)} %get-tuple-element.163, s32[]{:T(128)S(6)} %select_n.41), dynamic_slice_sizes={1} | dynamic-slice | bytes 12 | tf_op jit(solution)/shard_map/while/body/jit(dynamic_index_in_dim)/dynamic_slice | solution.py:22
  54.8 0.7 reduce-window.9
  55.5 1.2 %multiply_divide_fusion = (f32[8]{0:T(128)S(1)}, f32[8]{0:T(128)}) fusion(s32[]{:T(128)S(6)} %mul.1524, f32[8]{0:T(128)S(1)} %psum.7, f32[8,1]{0,1:T(1,128)} %reduce-window.9, f32[]{:T(128)S(6)} %add.521), kind=kLoop, calls=%fused_computation.325 | loop fusion | flops 88 | bytes 136 | tf_op jit(solution)/shard_map/div | solution.py:121
  57.1 0.8 multiply_multiply_fusion.3
  58.5 0.7 constant_dynamic-update-slice_fusion.23
  59.2 1.8 %subtract_multiply_fusion.1 = f32[8,8,16,129]{3,2,1,0:T(8,128)S(1)} fusion(f32[8,8,16,129]{3,2,1,0:T(8,128)S(1)} %get-tuple-element.87, f32[8,8,16,129]{3,2,1,0:T(8,128)S(1)} %get-tuple-element.86, f32[8,8,16,129]{3,2,1,0:T(8,128)} %get-tuple-element.116, f32[8,8,16,129]{3,2,1,0:T(8,128)S(1)} %get-tuple-element.117, f32[8,16,129]{2,1,0:T(8,128)S(1)} %get-tuple-element.70, ...), kind=kLoop, calls=%fused_computation.24 | loop fusion | flops 792576 | bytes 2708484 | tf_op jit(solution)/shard_map/mul | solution.py:109
  61.0 0.9 copy.630
  61.9 0.9 copy.631
  63.1 1.9 %collective-permute-start.3 = (f32[8,2,20,128]{3,0,2,1:T(8,128)S(1)}, f32[8,2,20,128]{3,0,2,1:T(8,128)S(1)}, u32[]{:S(2)}, u32[]{:S(2)}) collective-permute-start(f32[8,2,20,128]{3,0,2,1:T(8,128)S(1)} %copy.638), channel_id=1, source_target_pairs={{4,0},{8,4},{12,8},{16,12},{20,16},{24,20},{28,24},{5,1},{9,5},{13... | collective-permute-start | bytes 491528 | tf_op jit(solution)/shard_map/ppermute | solution.py:35
  65.1 4.7 %collective-permute-start.2 = (f32[8,2,20,128]{3,0,2,1:T(8,128)S(1)}, f32[8,2,20,128]{3,0,2,1:T(8,128)S(1)}, u32[]{:S(2)}, u32[]{:S(2)}) collective-permute-start(f32[8,2,20,128]{3,0,2,1:T(8,128)S(1)} %copy.634), channel_id=1, source_target_pairs={{0,4},{4,8},{8,12},{12,16},{16,20},{20,24},{24,28},{1,5},{5,9},{9,... | collective-permute-start | bytes 491528 | tf_op jit(solution)/shard_map/ppermute | solution.py:34
  69.8 0.6 minimum_multiply_fusion.3
  70.4 0.3 fusion.10
  71.6 1.6 %collective-permute-done.2 = f32[8,2,20,128]{3,0,2,1:T(8,128)S(1)} collective-permute-done((f32[8,2,20,128]{3,0,2,1:T(8,128)S(1)}, f32[8,2,20,128]{3,0,2,1:T(8,128)S(1)}, u32[]{:S(2)}, u32[]{:S(2)}) %collective-permute-start.2) | collective-permute-done | bytes 163872 | tf_op jit(solution)/shard_map/ppermute | solution.py:34
  73.5 0.3 minimum_multiply_fusion.5
  74.6 0.5 copy-done.5
  75.0 0.4 fusion.28
  75.5 0.5 slice_reduce_fusion.1
  76.1 1.7 %collective-permute-start.5 = (f32[8,8,2,128]{3,1,2,0:T(8,128)S(1)}, f32[8,8,2,128]{3,1,2,0:T(8,128)S(1)}, u32[]{:S(2)}, u32[]{:S(2)}) collective-permute-start(f32[8,8,2,128]{3,1,2,0:T(8,128)S(1)} %copy.649), channel_id=1, source_target_pairs={{1,0},{2,1},{3,2},{0,3},{5,4},{6,5},{7,6},{4,7},{9,8},{10,9},{11,1... | collective-permute-start | bytes 196616 | tf_op jit(solution)/shard_map/ppermute | solution.py:35
  78.2 0.5 pad_maximum_fusion.7
  78.7 0.3 slice_subtract_fusion
  79.0 0.7 minimum_multiply_fusion
  79.8 0.8 fusion.4
  80.5 0.2 multiply_bitcast_fusion
  81.3 0.9 copy-done.4
  82.5 0.5 subtract_multiply_fusion
  83.5 3.8 %collective-permute-start.6 = (f32[8,2,20,128]{3,0,2,1:T(8,128)S(1)}, f32[8,2,20,128]{3,0,2,1:T(8,128)S(1)}, u32[]{:S(2)}, u32[]{:S(2)}) collective-permute-start(f32[8,2,20,128]{3,0,2,1:T(8,128)S(1)} %copy.654), channel_id=1, source_target_pairs={{0,4},{4,8},{8,12},{12,16},{16,20},{20,24},{24,28},{1,5},{5,9},{9,... | collective-permute-start | bytes 491528 | tf_op jit(solution)/shard_map/ppermute | solution.py:34
  87.4 2.9 %collective-permute-start.7 = (f32[8,2,20,128]{3,0,2,1:T(8,128)S(1)}, f32[8,2,20,128]{3,0,2,1:T(8,128)S(1)}, u32[]{:S(2)}, u32[]{:S(2)}) collective-permute-start(f32[8,2,20,128]{3,0,2,1:T(8,128)S(1)} %copy.658), channel_id=1, source_target_pairs={{4,0},{8,4},{12,8},{16,12},{20,16},{24,20},{28,24},{5,1},{9,5},{13... | collective-permute-start | bytes 491528 | tf_op jit(solution)/shard_map/ppermute | solution.py:35
  90.3 0.6 minimum_multiply_fusion.2
  90.9 0.3 fusion.8
  92.0 0.6 collective-permute-done.6
  92.6 3.4 %collective-permute-done.7 = f32[8,2,20,128]{3,0,2,1:T(8,128)S(1)} collective-permute-done((f32[8,2,20,128]{3,0,2,1:T(8,128)S(1)}, f32[8,2,20,128]{3,0,2,1:T(8,128)S(1)}, u32[]{:S(2)}, u32[]{:S(2)}) %collective-permute-start.7) | collective-permute-done | bytes 163872 | tf_op jit(solution)/shard_map/ppermute | solution.py:35
  96.3 0.3 minimum_multiply_fusion.4
  97.4 1.2 %fusion.32 = f32[8,8,16,128]{3,2,1,0:T(8,128)} fusion(f32[8,8,16,128]{3,2,1,0:T(8,128)S(1)} %copy-done, f32[8,8,16,128]{3,2,1,0:T(8,128)S(1)} %fusion.28, f32[8,8,16,128]{3,2,1,0:T(8,128)S(1)} %constant_dynamic-update-slice_fusion.55, f32[8,8,17,128]{3,2,1,0:T(8,128)S(1)} %multiply_subtract_fusion, f32[8,8,16,129]{3,2,1,0:T(8,128)S(1)} %subtract_multiply_fusion, ...), kind=kLoop, calls=%fused_computation.97 | loop fusion | flops 1703936 | bytes 5251104 | tf_op jit(solution)/shard_map/add | solution.py:207
  (166 shorter events, 6.9 us)
Async XLA Ops:
  0.6 5.2 %copy-start = (f32[8,8,16,128]{3,2,1,0:T(8,128)S(1)}, f32[8,8,16,128]{3,2,1,0:T(8,128)}, u32[]{:S(2)}) copy-start(f32[8,8,16,128]{3,2,1,0:T(8,128)} %param.4) | copy-start | bytes 1572868
  2.4 58.6 %collective-permute-start = (f32[8,8,2,128]{3,1,2,0:T(8,128)}, f32[8,8,2,128]{3,1,2,0:T(8,128)}, u32[]{:S(2)}, u32[]{:S(2)}) collective-permute-start(f32[8,8,2,128]{3,1,2,0:T(8,128)} %copy.673), channel_id=1, source_target_pairs={{0,1},{1,2},{2,3},{3,0},{4,5},{5,6},{6,7},{7,4},{8,9},{9,10},{10,1... | collective-permute-start | bytes 196616 | tf_op jit(solution)/shard_map/ppermute | solution.py:34
  3.0 58.9 %collective-permute-start.1 = (f32[8,8,2,128]{3,1,2,0:T(8,128)}, f32[8,8,2,128]{3,1,2,0:T(8,128)}, u32[]{:S(2)}, u32[]{:S(2)}) collective-permute-start(f32[8,8,2,128]{3,1,2,0:T(8,128)} %copy.674), channel_id=1, source_target_pairs={{1,0},{2,1},{3,2},{0,3},{5,4},{6,5},{7,6},{4,7},{9,8},{10,9},{11,1... | collective-permute-start | bytes 196616 | tf_op jit(solution)/shard_map/ppermute | solution.py:35
  11.6 1.0 copy-start.1
  12.6 1.0 %copy-start.3 = (f32[8,8,16,129]{3,2,1,0:T(8,128)}, f32[8,8,16,129]{3,2,1,0:T(8,128)S(1)}, u32[]{:S(2)}) copy-start(f32[8,8,16,129]{3,2,1,0:T(8,128)S(1)} %constant_dynamic-update-slice_fusion.24) | copy-start | bytes 1585156
  55.5 3.0 %copy-start.2 = (f32[8,8,16,129]{3,2,1,0:T(8,128)S(1)}, f32[8,8,16,129]{3,2,1,0:T(8,128)}, u32[]{:S(2)}) copy-start(f32[8,8,16,129]{3,2,1,0:T(8,128)} %copy-done.1) | copy-start | bytes 1585156
  59.2 1.8 %copy-start.6 = (f32[8]{0:T(128)S(1)}, f32[8]{0:T(128)}, u32[]{:S(2)}) copy-start(f32[8]{0:T(128)} %broadcast_add_fusion) | copy-start | bytes 100
  63.1 8.4 %collective-permute-start.3 = (f32[8,2,20,128]{3,0,2,1:T(8,128)S(1)}, f32[8,2,20,128]{3,0,2,1:T(8,128)S(1)}, u32[]{:S(2)}, u32[]{:S(2)}) collective-permute-start(f32[8,2,20,128]{3,0,2,1:T(8,128)S(1)} %copy.638), channel_id=1, source_target_pairs={{4,0},{8,4},{12,8},{16,12},{20,16},{24,20},{28,24},{5,1},{9,5},{13... | collective-permute-start | bytes 491528 | tf_op jit(solution)/shard_map/ppermute | solution.py:35
  65.1 8.1 %collective-permute-start.2 = (f32[8,2,20,128]{3,0,2,1:T(8,128)S(1)}, f32[8,2,20,128]{3,0,2,1:T(8,128)S(1)}, u32[]{:S(2)}, u32[]{:S(2)}) collective-permute-start(f32[8,2,20,128]{3,0,2,1:T(8,128)S(1)} %copy.634), channel_id=1, source_target_pairs={{0,4},{4,8},{8,12},{12,16},{16,20},{20,24},{24,28},{1,5},{5,9},{9,... | collective-permute-start | bytes 491528 | tf_op jit(solution)/shard_map/ppermute | solution.py:34
  74.4 0.7 copy-start.5
  76.0 7.1 %collective-permute-start.4 = (f32[8,8,2,128]{3,1,2,0:T(8,128)S(1)}, f32[8,8,2,128]{3,1,2,0:T(8,128)S(1)}, u32[]{:S(2)}, u32[]{:S(2)}) collective-permute-start(f32[8,8,2,128]{3,1,2,0:T(8,128)S(1)} %copy.648), channel_id=1, source_target_pairs={{0,1},{1,2},{2,3},{3,0},{4,5},{5,6},{6,7},{7,4},{8,9},{9,10},{10,1... | collective-permute-start | bytes 196616 | tf_op jit(solution)/shard_map/ppermute | solution.py:34
  76.1 7.0 %collective-permute-start.5 = (f32[8,8,2,128]{3,1,2,0:T(8,128)S(1)}, f32[8,8,2,128]{3,1,2,0:T(8,128)S(1)}, u32[]{:S(2)}, u32[]{:S(2)}) collective-permute-start(f32[8,8,2,128]{3,1,2,0:T(8,128)S(1)} %copy.649), channel_id=1, source_target_pairs={{1,0},{2,1},{3,2},{0,3},{5,4},{6,5},{7,6},{4,7},{9,8},{10,9},{11,1... | collective-permute-start | bytes 196616 | tf_op jit(solution)/shard_map/ppermute | solution.py:35
  81.1 1.0 %copy-start.4 = (f32[8,8,16,128]{3,2,1,0:T(8,128)S(1)}, f32[8,8,16,128]{3,2,1,0:T(8,128)}, u32[]{:S(2)}) copy-start(f32[8,8,16,128]{3,2,1,0:T(8,128)} %constant_dynamic-update-slice_fusion.61) | copy-start | bytes 1572868
  83.5 9.1 %collective-permute-start.6 = (f32[8,2,20,128]{3,0,2,1:T(8,128)S(1)}, f32[8,2,20,128]{3,0,2,1:T(8,128)S(1)}, u32[]{:S(2)}, u32[]{:S(2)}) collective-permute-start(f32[8,2,20,128]{3,0,2,1:T(8,128)S(1)} %copy.654), channel_id=1, source_target_pairs={{0,4},{4,8},{8,12},{12,16},{16,20},{20,24},{24,28},{1,5},{5,9},{9,... | collective-permute-start | bytes 491528 | tf_op jit(solution)/shard_map/ppermute | solution.py:34
  87.4 8.6 %collective-permute-start.7 = (f32[8,2,20,128]{3,0,2,1:T(8,128)S(1)}, f32[8,2,20,128]{3,0,2,1:T(8,128)S(1)}, u32[]{:S(2)}, u32[]{:S(2)}) collective-permute-start(f32[8,2,20,128]{3,0,2,1:T(8,128)S(1)} %copy.658), channel_id=1, source_target_pairs={{4,0},{8,4},{12,8},{16,12},{20,16},{24,20},{28,24},{5,1},{9,5},{13... | collective-permute-start | bytes 491528 | tf_op jit(solution)/shard_map/ppermute | solution.py:35
where the time goes:
time: 99.2 us; the launch traced here: 98.6 us
  blocking collectives  23.2 us (23%)
  local copies, waits for them, and re-layouts  22.9 us (23%)
  other arithmetic  22.4 us (23%)
  starting transfers between devices  16.9 us (17%)
  waiting for transfers between devices  5.66 us (6%)
  loops' own time  3.87 us (4%)
  between operations  3 us (3%)
    unnamed x1, blocking collectives  17.5 us
    unnamed x25, local copies, waits for them, and re-layouts  10.1 us
    ppermute x4, starting transfers between devices, extended_2(): before = lax.ppermute(last, axis, up)  8.58 us
    ppermute x4, starting transfers between devices, extended_2(): after = lax.ppermute(initial, axis, down)  8.32 us
    dynamic_slice x6, local copies, waits for them, and re-layouts, one(): return combine(state, lax.dynamic_index_in_dim(gathered, lap, 0, False))  7.39 us
    psum x1, blocking collectives, body(): shells = lax.psum(local_shells, 'phi')  5.76 us
    another operation x1, loops' own time, entering(): return lax.fori_loop(0, place, one, state)  3.87 us
    ppermute x4, waiting for transfers between devices, extended_2(): after = lax.ppermute(initial, axis, down)  3.39 us
  transfers between devices with their start and end apart: 8, of which 3 were waited for; matrix products, arithmetic and copies ran while one was open for 35% of the time, Pallas kernels for 0%

commit v1 on v0

--- a/solution.py
+++ b/solution.py
@@ -1,3 +1,4 @@
+import functools
 import math
 import jax
 import jax.numpy as jnp
@@ -11,6 +12,13 @@
 GRAVITY_KICK = 0.004
 MINIMUM_DENSITY = 0.05
 PRESSURE_FLOOR = 0.01
+
+
+def wrap_terms_on(mine, row_axis):
+    return jax.lax.all_gather(mine, axis_name=row_axis).sum(axis=0)
+
+
+loads_edit = functools.partial(wrap_terms_on, row_axis="phi")
 
 
 def entering(part, axis, combine, identity):
@@ -172,7 +180,7 @@
     local_shells = (
         local_shells * cell_centers * cell_centers * (radial_step * theta_step * phi_step)
     )
-    shells = lax.psum(local_shells, "phi")
+    shells = loads_edit(local_shells)
     before = entering(jnp.sum(shells), "radial", add_terms, jnp.float32(0.0))
     enclosed = core_mass[0] + before + jnp.cumsum(shells) - 0.5 * shells
 

time: 99.2 us -> 99.4 us (level)
    psum x1 -> x0, blocking collectives: 5.76 us -> none  [body(): shells = lax.psum(local_shells, 'phi')]
    unnamed x1 -> x2, blocking collectives: 17.5 us -> 23.1 us
    unnamed x25 -> x32, local copies, waits for them, and re-layouts: 10.1 us -> 10.2 us
where the time goes in v1:
time: 99.4 us; the launch traced here: 98.8 us
  blocking collectives  23.1 us (23%)
  other arithmetic  23 us (23%)
  local copies, waits for them, and re-layouts  22.7 us (23%)
  starting transfers between devices  16.8 us (17%)
  waiting for transfers between devices  5.8 us (6%)
  between operations  3.87 us (4%)
  loops' own time  3.43 us (3%)
    unnamed x2, blocking collectives  23.1 us
    unnamed x32, local copies, waits for them, and re-layouts  10.2 us
    ppermute x4, starting transfers between devices, extended_2(): after = lax.ppermute(initial, axis, down)  8.46 us
    ppermute x4, starting transfers between devices, extended_2(): before = lax.ppermute(last, axis, up)  8.3 us
    dynamic_slice x6, local copies, waits for them, and re-layouts, one(): return combine(state, lax.dynamic_index_in_dim(gathered, lap, 0, False))  6.97 us
    another operation x1, loops' own time, entering(): return lax.fori_loop(0, place, one, state)  3.43 us
    ppermute x4, waiting for transfers between devices, extended_2(): after = lax.ppermute(initial, axis, down)  3.38 us
    mul x6, other arithmetic, face_flux(): 0.5 * (jnp.sign(below_diff) + jnp.sign(above_diff))  3.14 us
  transfers between devices with their start and end apart: 8, of which 3 were waited for; matrix products, arithmetic and copies ran while one was open for 35% of the time, Pallas kernels for 0%

profile of v1, /device:TPU:24, one launch (start us, length us, event | category | flops | bytes accessed | tf_op | source)
XLA Modules:
  0.0 98.8 jit_solution(5330379107083946815)
XLA Ops:
  0.6 1.1 %fusion.53 = (f32[8,8,2,128]{3,2,1,0:T(2,128)S(1)}, f32[8,8,2,128]{3,2,1,0:T(2,128)S(1)}) fusion(f32[8,8,16,128]{3,2,1,0:T(8,128)} %param.4), kind=kLoop, calls=%fused_computation.338 | loop fusion | bytes 262144 | tf_op jit(solution)/shard_map/slice | solution.py:40
  1.8 0.6 copy.673
  2.4 0.6 copy.674
  3.0 1.7 %collective-permute-start.1 = (f32[8,8,2,128]{3,1,2,0:T(8,128)}, f32[8,8,2,128]{3,1,2,0:T(8,128)}, u32[]{:S(2)}, u32[]{:S(2)}) collective-permute-start(f32[8,8,2,128]{3,1,2,0:T(8,128)} %copy.674), channel_id=1, source_target_pairs={{1,0},{2,1},{3,2},{0,3},{5,4},{6,5},{7,6},{4,7},{9,8},{10,9},{11,1... | collective-permute-start | bytes 196616 | tf_op jit(solution)/shard_map/ppermute | solution.py:43
  4.8 0.6 multiply_multiply_fusion.4
  5.4 0.6 broadcast_add_fusion
  6.4 0.6 dynamic-slice
  7.7 0.2 dynamic-update-slice
  7.9 5.6 %all-reduce = f32[32]{0:T(128)S(1)} all-reduce(f32[32]{0:T(128)S(1)} %dynamic-update-slice), channel_id=2, replica_groups=mesh['radial'=8,'phi'=4] {'phi'}, use_global_device_ids=true, to_apply=%add | all-reduce | flops 32 | bytes 256
  13.5 0.7 reduce_sum.28
  14.4 0.6 fusion.44
  14.9 0.6 constant_dynamic-update-slice_fusion.61
  15.6 0.4 copy.675
  16.0 0.4 copy.676
  16.9 0.5 pad_maximum_fusion.6
  17.3 0.3 slice_subtract_fusion.1
  17.7 0.7 minimum_multiply_fusion.1
  18.4 0.8 fusion.6
  19.9 0.8 copy-done.1
  20.7 1.0 %copy-done.3 = f32[8,8,16,129]{3,2,1,0:T(8,128)} copy-done((f32[8,8,16,129]{3,2,1,0:T(8,128)}, f32[8,8,16,129]{3,2,1,0:T(8,128)S(1)}, u32[]{:S(2)}) %copy-start.3) | copy-done | bytes 528408
  21.6 0.6 dynamic-slice.1
  22.2 0.5 broadcast.580
  22.7 2.4 %dynamic-update-slice.1 = f32[8]{0:T(128)} dynamic-update-slice(f32[8]{0:T(128)} %broadcast.580, f32[1]{0:T(128)} %bitcast.5, u32[]{:T(128)} %bitcast.6) | dynamic-update-slice | bytes 12
  25.1 0.7 slice.710
  25.8 17.4 %all-reduce.1 = f32[8]{0:T(128)} all-reduce(f32[8]{0:T(128)} %dynamic-update-slice.1), channel_id=1, replica_groups=mesh['radial'=8,'phi'=4] {'radial'}, use_global_device_ids=true, to_apply=%add.1 | all-reduce | flops 8 | bytes 64
  43.2 10.4 %while.10 = (s32[]{:T(128)}, f32[]{:T(128)}, s32[]{:T(128)}, f32[8]{0:T(128)}, s32[]{:T(128)}, /*index=5*/s32[]{:T(128)}, s32[]{:T(128)}) while((s32[]{:T(128)}, f32[]{:T(128)}, s32[]{:T(128)}, f32[8]{0:T(128)}, s32[]{:T(128)}, /*index=5*/s32[]{:T(128)}, s32[]{:T(128)}) %tuple.74), condition=%wide.region_3.4_spmd, body=%wide.region_2.0_spmd.sunk | while | flops 6 | bytes 135 | solution.py:32
  43.2 1.2 %dynamic_slice.5 = f32[1]{0:T(128)} dynamic-slice(f32[8]{0:T(128)} %get-tuple-element.163, s32[]{:T(128)S(6)} %select_n.41), dynamic_slice_sizes={1} | dynamic-slice | bytes 12 | tf_op jit(solution)/shard_map/while/body/jit(dynamic_index_in_dim)/dynamic_slice | solution.py:30
  44.9 1.2 %dynamic_slice.5 = f32[1]{0:T(128)} dynamic-slice(f32[8]{0:T(128)} %get-tuple-element.163, s32[]{:T(128)S(6)} %select_n.41), dynamic_slice_sizes={1} | dynamic-slice | bytes 12 | tf_op jit(solution)/shard_map/while/body/jit(dynamic_index_in_dim)/dynamic_slice | solution.py:30
  46.7 1.2 %dynamic_slice.5 = f32[1]{0:T(128)} dynamic-slice(f32[8]{0:T(128)} %get-tuple-element.163, s32[]{:T(128)S(6)} %select_n.41), dynamic_slice_sizes={1} | dynamic-slice | bytes 12 | tf_op jit(solution)/shard_map/while/body/jit(dynamic_index_in_dim)/dynamic_slice | solution.py:30
  48.4 1.2 %dynamic_slice.5 = f32[1]{0:T(128)} dynamic-slice(f32[8]{0:T(128)} %get-tuple-element.163, s32[]{:T(128)S(6)} %select_n.41), dynamic_slice_sizes={1} | dynamic-slice | bytes 12 | tf_op jit(solution)/shard_map/while/body/jit(dynamic_index_in_dim)/dynamic_slice | solution.py:30
  50.2 1.2 %dynamic_slice.5 = f32[1]{0:T(128)} dynamic-slice(f32[8]{0:T(128)} %get-tuple-element.163, s32[]{:T(128)S(6)} %select_n.41), dynamic_slice_sizes={1} | dynamic-slice | bytes 12 | tf_op jit(solution)/shard_map/while/body/jit(dynamic_index_in_dim)/dynamic_slice | solution.py:30
  51.9 1.2 %dynamic_slice.5 = f32[1]{0:T(128)} dynamic-slice(f32[8]{0:T(128)} %get-tuple-element.163, s32[]{:T(128)S(6)} %select_n.41), dynamic_slice_sizes={1} | dynamic-slice | bytes 12 | tf_op jit(solution)/shard_map/while/body/jit(dynamic_index_in_dim)/dynamic_slice | solution.py:30
  54.3 0.5 reduce_sum.29
  54.8 0.8 reduce-window.7
  55.6 1.3 %multiply_divide_fusion = (f32[8]{0:T(128)S(1)}, f32[8]{0:T(128)}) fusion(s32[]{:T(128)S(6)} %mul.1540, f32[8]{0:T(128)} %reduce_sum.29, f32[8,1]{0,1:T(1,128)S(1)} %reduce-window.7, f32[]{:T(128)S(6)} %add.535), kind=kLoop, calls=%fused_computation.325 | loop fusion | flops 88 | bytes 136 | tf_op jit(solution)/shard_map/div | solution.py:129
  57.3 0.7 multiply_multiply_fusion.3
  58.6 0.7 constant_dynamic-update-slice_fusion.23
  59.3 1.8 %subtract_multiply_fusion.1 = f32[8,8,16,129]{3,2,1,0:T(8,128)S(1)} fusion(f32[8,8,16,129]{3,2,1,0:T(8,128)S(1)} %get-tuple-element.87, f32[8,8,16,129]{3,2,1,0:T(8,128)S(1)} %get-tuple-element.86, f32[8,8,16,129]{3,2,1,0:T(8,128)} %get-tuple-element.116, f32[8,8,16,129]{3,2,1,0:T(8,128)S(1)} %get-tuple-element.117, f32[8,16,129]{2,1,0:T(8,128)S(1)} %get-tuple-element.70, ...), kind=kLoop, calls=%fused_computation.24 | loop fusion | flops 792576 | bytes 2708484 | tf_op jit(solution)/shard_map/mul | solution.py:117
  61.2 0.9 copy.630
  62.1 0.9 copy.631
  63.3 1.9 %collective-permute-start.3 = (f32[8,2,20,128]{3,0,2,1:T(8,128)S(1)}, f32[8,2,20,128]{3,0,2,1:T(8,128)S(1)}, u32[]{:S(2)}, u32[]{:S(2)}) collective-permute-start(f32[8,2,20,128]{3,0,2,1:T(8,128)S(1)} %copy.638), channel_id=1, source_target_pairs={{4,0},{8,4},{12,8},{16,12},{20,16},{24,20},{28,24},{5,1},{9,5},{13... | collective-permute-start | bytes 491528 | tf_op jit(solution)/shard_map/ppermute | solution.py:43
  65.3 4.6 %collective-permute-start.2 = (f32[8,2,20,128]{3,0,2,1:T(8,128)S(1)}, f32[8,2,20,128]{3,0,2,1:T(8,128)S(1)}, u32[]{:S(2)}, u32[]{:S(2)}) collective-permute-start(f32[8,2,20,128]{3,0,2,1:T(8,128)S(1)} %copy.634), channel_id=1, source_target_pairs={{0,4},{4,8},{8,12},{12,16},{16,20},{20,24},{24,28},{1,5},{5,9},{9,... | collective-permute-start | bytes 491528 | tf_op jit(solution)/shard_map/ppermute | solution.py:42
  69.8 0.6 minimum_multiply_fusion.3
  70.4 0.3 fusion.10
  71.5 1.8 %collective-permute-done.2 = f32[8,2,20,128]{3,0,2,1:T(8,128)S(1)} collective-permute-done((f32[8,2,20,128]{3,0,2,1:T(8,128)S(1)}, f32[8,2,20,128]{3,0,2,1:T(8,128)S(1)}, u32[]{:S(2)}, u32[]{:S(2)}) %collective-permute-start.2) | collective-permute-done | bytes 163872 | tf_op jit(solution)/shard_map/ppermute | solution.py:42
  73.7 0.3 minimum_multiply_fusion.5
  74.8 0.5 copy-done.5
  75.2 0.4 fusion.28
  75.7 0.5 slice_reduce_fusion.1
  76.3 1.7 %collective-permute-start.5 = (f32[8,8,2,128]{3,1,2,0:T(8,128)S(1)}, f32[8,8,2,128]{3,1,2,0:T(8,128)S(1)}, u32[]{:S(2)}, u32[]{:S(2)}) collective-permute-start(f32[8,8,2,128]{3,1,2,0:T(8,128)S(1)} %copy.649), channel_id=1, source_target_pairs={{1,0},{2,1},{3,2},{0,3},{5,4},{6,5},{7,6},{4,7},{9,8},{10,9},{11,1... | collective-permute-start | bytes 196616 | tf_op jit(solution)/shard_map/ppermute | solution.py:43
  78.4 0.5 pad_maximum_fusion.7
  78.9 0.3 slice_subtract_fusion
  79.2 0.7 minimum_multiply_fusion
  79.9 0.7 fusion.4
  81.4 0.9 copy-done.4
  82.7 0.5 subtract_multiply_fusion
  83.7 3.7 %collective-permute-start.6 = (f32[8,2,20,128]{3,0,2,1:T(8,128)S(1)}, f32[8,2,20,128]{3,0,2,1:T(8,128)S(1)}, u32[]{:S(2)}, u32[]{:S(2)}) collective-permute-start(f32[8,2,20,128]{3,0,2,1:T(8,128)S(1)} %copy.654), channel_id=1, source_target_pairs={{0,4},{4,8},{8,12},{12,16},{16,20},{20,24},{24,28},{1,5},{5,9},{9,... | collective-permute-start | bytes 491528 | tf_op jit(solution)/shard_map/ppermute | solution.py:42
  87.4 3.1 %collective-permute-start.7 = (f32[8,2,20,128]{3,0,2,1:T(8,128)S(1)}, f32[8,2,20,128]{3,0,2,1:T(8,128)S(1)}, u32[]{:S(2)}, u32[]{:S(2)}) collective-permute-start(f32[8,2,20,128]{3,0,2,1:T(8,128)S(1)} %copy.658), channel_id=1, source_target_pairs={{4,0},{8,4},{12,8},{16,12},{20,16},{24,20},{28,24},{5,1},{9,5},{13... | collective-permute-start | bytes 491528 | tf_op jit(solution)/shard_map/ppermute | solution.py:43
  90.5 0.6 minimum_multiply_fusion.2
  91.0 0.3 fusion.8
  92.2 0.6 collective-permute-done.6
  92.8 3.4 %collective-permute-done.7 = f32[8,2,20,128]{3,0,2,1:T(8,128)S(1)} collective-permute-done((f32[8,2,20,128]{3,0,2,1:T(8,128)S(1)}, f32[8,2,20,128]{3,0,2,1:T(8,128)S(1)}, u32[]{:S(2)}, u32[]{:S(2)}) %collective-permute-start.7) | collective-permute-done | bytes 163872 | tf_op jit(solution)/shard_map/ppermute | solution.py:43
  96.5 0.3 minimum_multiply_fusion.4
  97.5 1.2 %fusion.32 = f32[8,8,16,128]{3,2,1,0:T(8,128)} fusion(f32[8,8,16,128]{3,2,1,0:T(8,128)S(1)} %copy-done, f32[8,8,16,128]{3,2,1,0:T(8,128)S(1)} %fusion.28, f32[8,8,16,128]{3,2,1,0:T(8,128)S(1)} %constant_dynamic-update-slice_fusion.55, f32[8,8,17,128]{3,2,1,0:T(8,128)S(1)} %multiply_subtract_fusion, f32[8,8,16,129]{3,2,1,0:T(8,128)S(1)} %subtract_multiply_fusion, ...), kind=kLoop, calls=%fused_computation.97 | loop fusion | flops 1703936 | bytes 5251104 | tf_op jit(solution)/shard_map/add | solution.py:215
  (175 shorter events, 7.6 us)
Async XLA Ops:
  0.6 5.3 %copy-start = (f32[8,8,16,128]{3,2,1,0:T(8,128)S(1)}, f32[8,8,16,128]{3,2,1,0:T(8,128)}, u32[]{:S(2)}) copy-start(f32[8,8,16,128]{3,2,1,0:T(8,128)} %param.4) | copy-start | bytes 1572868
  2.4 4.0 %copy-start.8 = (u32[32]{0:T(128)S(1)}, u32[32]{0:T(128)}, u32[]{:S(2)}) copy-start(u32[32]{0:T(128)} %constant.10) | copy-start | bytes 388
  2.4 58.8 %collective-permute-start = (f32[8,8,2,128]{3,1,2,0:T(8,128)}, f32[8,8,2,128]{3,1,2,0:T(8,128)}, u32[]{:S(2)}, u32[]{:S(2)}) collective-permute-start(f32[8,8,2,128]{3,1,2,0:T(8,128)} %copy.673), channel_id=1, source_target_pairs={{0,1},{1,2},{2,3},{3,0},{4,5},{5,6},{6,7},{7,4},{8,9},{9,10},{10,1... | collective-permute-start | bytes 196616 | tf_op jit(solution)/shard_map/ppermute | solution.py:42
  3.0 59.0 %collective-permute-start.1 = (f32[8,8,2,128]{3,1,2,0:T(8,128)}, f32[8,8,2,128]{3,1,2,0:T(8,128)}, u32[]{:S(2)}, u32[]{:S(2)}) collective-permute-start(f32[8,8,2,128]{3,1,2,0:T(8,128)} %copy.674), channel_id=1, source_target_pairs={{1,0},{2,1},{3,2},{0,3},{5,4},{6,5},{7,6},{4,7},{9,8},{10,9},{11,1... | collective-permute-start | bytes 196616 | tf_op jit(solution)/shard_map/ppermute | solution.py:43
  19.6 1.0 copy-start.1
  19.7 1.9 %copy-start.7 = (u32[32]{0:T(128)S(1)}, u32[32]{0:T(128)}, u32[]{:S(2)}) copy-start(u32[32]{0:T(128)} %constant.15) | copy-start | bytes 388
  20.6 1.0 %copy-start.3 = (f32[8,8,16,129]{3,2,1,0:T(8,128)}, f32[8,8,16,129]{3,2,1,0:T(8,128)S(1)}, u32[]{:S(2)}) copy-start(f32[8,8,16,129]{3,2,1,0:T(8,128)S(1)} %constant_dynamic-update-slice_fusion.24) | copy-start | bytes 1585156
  55.6 3.0 %copy-start.2 = (f32[8,8,16,129]{3,2,1,0:T(8,128)S(1)}, f32[8,8,16,129]{3,2,1,0:T(8,128)}, u32[]{:S(2)}) copy-start(f32[8,8,16,129]{3,2,1,0:T(8,128)} %copy-done.1) | copy-start | bytes 1585156
  59.3 1.8 %copy-start.6 = (f32[8]{0:T(128)S(1)}, f32[8]{0:T(128)}, u32[]{:S(2)}) copy-start(f32[8]{0:T(128)} %broadcast_add_fusion) | copy-start | bytes 100
  63.3 8.2 %collective-permute-start.3 = (f32[8,2,20,128]{3,0,2,1:T(8,128)S(1)}, f32[8,2,20,128]{3,0,2,1:T(8,128)S(1)}, u32[]{:S(2)}, u32[]{:S(2)}) collective-permute-start(f32[8,2,20,128]{3,0,2,1:T(8,128)S(1)} %copy.638), channel_id=1, source_target_pairs={{4,0},{8,4},{12,8},{16,12},{20,16},{24,20},{28,24},{5,1},{9,5},{13... | collective-permute-start | bytes 491528 | tf_op jit(solution)/shard_map/ppermute | solution.py:43
  65.3 8.1 %collective-permute-start.2 = (f32[8,2,20,128]{3,0,2,1:T(8,128)S(1)}, f32[8,2,20,128]{3,0,2,1:T(8,128)S(1)}, u32[]{:S(2)}, u32[]{:S(2)}) collective-permute-start(f32[8,2,20,128]{3,0,2,1:T(8,128)S(1)} %copy.634), channel_id=1, source_target_pairs={{0,4},{4,8},{8,12},{12,16},{16,20},{20,24},{24,28},{1,5},{5,9},{9,... | collective-permute-start | bytes 491528 | tf_op jit(solution)/shard_map/ppermute | solution.py:42
  74.6 0.7 copy-start.5
  76.2 7.0 %collective-permute-start.4 = (f32[8,8,2,128]{3,1,2,0:T(8,128)S(1)}, f32[8,8,2,128]{3,1,2,0:T(8,128)S(1)}, u32[]{:S(2)}, u32[]{:S(2)}) collective-permute-start(f32[8,8,2,128]{3,1,2,0:T(8,128)S(1)} %copy.648), channel_id=1, source_target_pairs={{0,1},{1,2},{2,3},{3,0},{4,5},{5,6},{6,7},{7,4},{8,9},{9,10},{10,1... | collective-permute-start | bytes 196616 | tf_op jit(solution)/shard_map/ppermute | solution.py:42
  76.3 7.0 %collective-permute-start.5 = (f32[8,8,2,128]{3,1,2,0:T(8,128)S(1)}, f32[8,8,2,128]{3,1,2,0:T(8,128)S(1)}, u32[]{:S(2)}, u32[]{:S(2)}) collective-permute-start(f32[8,8,2,128]{3,1,2,0:T(8,128)S(1)} %copy.649), channel_id=1, source_target_pairs={{1,0},{2,1},{3,2},{0,3},{5,4},{6,5},{7,6},{4,7},{9,8},{10,9},{11,1... | collective-permute-start | bytes 196616 | tf_op jit(solution)/shard_map/ppermute | solution.py:43
  81.3 1.0 %copy-start.4 = (f32[8,8,16,128]{3,2,1,0:T(8,128)S(1)}, f32[8,8,16,128]{3,2,1,0:T(8,128)}, u32[]{:S(2)}) copy-start(f32[8,8,16,128]{3,2,1,0:T(8,128)} %constant_dynamic-update-slice_fusion.61) | copy-start | bytes 1572868
  83.7 9.1 %collective-permute-start.6 = (f32[8,2,20,128]{3,0,2,1:T(8,128)S(1)}, f32[8,2,20,128]{3,0,2,1:T(8,128)S(1)}, u32[]{:S(2)}, u32[]{:S(2)}) collective-permute-start(f32[8,2,20,128]{3,0,2,1:T(8,128)S(1)} %copy.654), channel_id=1, source_target_pairs={{0,4},{4,8},{8,12},{12,16},{16,20},{20,24},{24,28},{1,5},{5,9},{9,... | collective-permute-start | bytes 491528 | tf_op jit(solution)/shard_map/ppermute | solution.py:42
  87.4 8.8 %collective-permute-start.7 = (f32[8,2,20,128]{3,0,2,1:T(8,128)S(1)}, f32[8,2,20,128]{3,0,2,1:T(8,128)S(1)}, u32[]{:S(2)}, u32[]{:S(2)}) collective-permute-start(f32[8,2,20,128]{3,0,2,1:T(8,128)S(1)} %copy.658), channel_id=1, source_target_pairs={{4,0},{8,4},{12,8},{16,12},{20,16},{24,20},{28,24},{5,1},{9,5},{13... | collective-permute-start | bytes 491528 | tf_op jit(solution)/shard_map/ppermute | solution.py:43
